TPU v7x, 8 devices: a whole 2x2x1 slice. The times are simulated.
8 devices in a mesh: dp: 1 (over z), tp: 2 (over y), ep: 4 (over x, core).
Axes of the slice: x: 2, y: 2, z: 1, core: 2. Of those that a mesh axis runs over, the one named last changes fastest.
Arguments:
- hidden_in: bfloat16 [32, 256, 1024], P(('dp', 'ep'), 'tp')
- ln_attn: float32 [2, 1024], replicated
- ln_ffn: float32 [2, 1024], replicated
- w_query: bfloat16 [2, 1024, 1024], P(None, None, 'tp')
- w_key: bfloat16 [2, 1024, 1024], P(None, None, 'tp')
- w_value: bfloat16 [2, 1024, 1024], P(None, None, 'tp')
- w_out: bfloat16 [2, 1024, 1024], P(None, 'tp')
- bias_table: float32 [2, 16, 32], P(None, 'tp')
- w_gate: bfloat16 [1024, 512], P(None, 'tp')
- w_up: bfloat16 [1024, 512], P(None, 'tp')
- w_down: bfloat16 [512, 1024], P('tp')
- w_router: float32 [1024, 32], replicated
- expert_in: bfloat16 [32, 1024, 512], P(('tp', 'ep'))
- expert_out: bfloat16 [32, 512, 1024], P(('tp', 'ep'))
- expert_ids: int32 [32, 256, 2], P(('dp', 'ep'), 'tp')
Outputs:
- output 1: bfloat16 [32, 256, 1024], P(('dp', 'ep'), 'tp')
- output 2: bfloat16 [2, 32, 16, 256, 64], P(None, ('dp', 'ep'), 'tp')
- output 3: bfloat16 [2, 32, 16, 256, 64], P(None, ('dp', 'ep'), 'tp')
All inputs are finite; a program needn't handle non-finite values.
Results may differ from a plain program's by a relative error of at most 0.0146873.
Values are sent between devices in bfloat16 or wider.
A program may use at most 1 GiB of HBM per device.

v0:
```python
import contextlib

import jax
import jax.numpy as jnp
from jax import lax
from jax.experimental import pallas as pl
from jax.experimental.pallas import tpu as pltpu
from jax.sharding import PartitionSpec as P

EXACT_BUCKETS = 16
THRESHOLDS = (18, 20, 23, 26, 30, 34, 39, 45, 51, 58, 66, 76, 86, 98, 112)
EPSILON = 1e-6
F32 = jnp.float32
BF16 = jnp.bfloat16
VMEM_LIMIT = 60 * 1024 * 1024
MESH = pl.DeviceIdType.MESH


def scope(name):
    return contextlib.nullcontext()


def rms_rows(rows, ln_scale):
    wide = rows.astype(F32)
    inv_rms = lax.rsqrt(jnp.mean(wide * wide, axis=-1, keepdims=True) + EPSILON)
    return (wide * inv_rms * ln_scale).astype(BF16)


def mm(a, b):
    return lax.dot_general(a, b, (((1,), (0,)), ((), ())), preferred_element_type=F32)


def mm_t(a, b):
    return lax.dot_general(a, b, (((1,), (1,)), ((), ())), preferred_element_type=F32)


def bias_rows(table, seq_len):
    at = lax.broadcasted_iota(jnp.int32, (table.shape[1], 2 * seq_len), 1)
    rel = jnp.where(at == 0, 0, 2 * seq_len - at)
    bucket = jnp.minimum(rel, EXACT_BUCKETS)
    for threshold in THRESHOLDS:
        bucket = bucket + jnp.where(rel >= threshold, 1, 0)
    hot = jnp.where(bucket == lax.broadcasted_iota(jnp.int32, bucket.shape, 0), 1.0, 0.0)
    rows = jnp.dot(table, hot, precision=lax.Precision.HIGHEST, preferred_element_type=F32)
    return jnp.where(rel[:1] < seq_len, rows, -jnp.inf)


def softmax_bf16(scores):
    top = jnp.max(scores, axis=-1, keepdims=True)
    grown = jnp.exp(scores - top)
    return (grown * (1.0 / jnp.sum(grown, axis=-1, keepdims=True))).astype(BF16)


def axis_neighbours(tp, ep):
    core = lax.rem(ep, 2)
    beside = ep + 1 - 2 * core
    return beside, lax.rem(ep + 2, 4), lax.rem(beside + 2, 4)


def remote(src, dst, send, recv, tp, ep):
    return pltpu.make_async_remote_copy(
        src_ref=src, dst_ref=dst, send_sem=send, recv_sem=recv,
        device_id=(lax.axis_index('dp'), tp, ep), device_id_type=MESH)


def layers_body(hid_ref, ln_attn_ref, ln_ffn_ref, wq_hbm, wk_hbm, wv_hbm, wo_hbm, table_ref, wg_hbm, wu_hbm, wd_hbm,
                h1_ref, h2_ref, x0_ref, x0t_ref,
                x, a_ref, acc, w, wo, gu, wd, table_other, u_rows, bias_low, bias_high, qkv, ctx, stage,
                in_sem, own_sem, out_sem, x0_sem, entry_send, entry_recv, misc_send, misc_recv, y_send, y_recv, x_send, x_recv, c_send, c_recv, d_send, d_recv):
    tp, ep = lax.axis_index('tp'), lax.axis_index('ep')
    other = 1 - tp
    ep1, ep2, ep3 = axis_neighbours(tp, ep)
    seqs, seq_len, d_model = x.shape
    half = seq_len // 2
    tokens = seqs * seq_len
    quad = qkv.shape[2]

    def part(count, quarter):
        return pl.ds(pl.multiple_of(quarter * count, count), count)

    my_pos = part(half, tp)
    mine = hid_ref.at[pl.ds(tp * seqs, seqs)]
    theirs = hid_ref.at[pl.ds(other * seqs, seqs)]

    sources, places = [], []
    for layer in range(2):
        for kind, hbm in enumerate((wq_hbm, wk_hbm, wv_hbm)):
            sources.append(hbm.at[layer, part(256, ep), :])
            places.append(lambda q, layer=layer, kind=kind: w.at[layer, 1, kind, part(256, q), :])
        sources.append(wo_hbm.at[layer, part(128, ep), :])
        places.append(lambda q, layer=layer: wo.at[layer, 1, part(128, q), :])
        if layer == 0:
            for kind, hbm in enumerate((wg_hbm, wu_hbm)):
                sources.append(hbm.at[part(256, ep), :])
                places.append(lambda q, kind=kind: gu.at[1, kind, part(256, q), :])
            sources.append(wd_hbm.at[part(64, ep), :])
            places.append(lambda q: wd.at[1, part(64, q), :])

    own_x = pltpu.make_async_copy(mine, x.at[:, my_pos, :], in_sem.at[0])
    own_stage = pltpu.make_async_copy(theirs, stage, in_sem.at[1])
    own_x.start()
    own_loads = []
    for layer in range(2):
        for kind, hbm in enumerate((wq_hbm, wk_hbm, wv_hbm)):
            own_loads.append((hbm.at[layer], w.at[layer, 0, kind]))
        own_loads.append((wo_hbm.at[layer], wo.at[layer, 0]))
        if layer == 0:
            own_loads += [(wg_hbm, gu.at[0, 0]), (wu_hbm, gu.at[0, 1]), (wd_hbm, wd.at[0])]
    own_loads = [pltpu.make_async_copy(s, d, own_sem.at[n]) for n, (s, d) in enumerate(own_loads)]
    for load in own_loads:
        load.start()
    own_stage.start()

    barrier = pltpu.get_barrier_semaphore()
    for peer_tp, peer_ep in ((other, ep), (tp, ep2), (tp, ep1)):
        pl.semaphore_signal(barrier, inc=1, device_id=(lax.axis_index('dp'), peer_tp, peer_ep), device_id_type=MESH)
    pl.semaphore_wait(barrier, 3)

    def arrived(ref, sem):
        remote(ref, ref, misc_send.at[0], sem, tp, ep).wait_recv()

    pieces = range(len(sources))
    entry_copies = [remote(hid_ref.at[other * seqs + s], x.at[s, my_pos, :], entry_send.at[s], entry_recv.at[s], other, ep) for s in range(seqs)]
    send_u = remote(table_ref, table_other, misc_send.at[1], misc_recv.at[1], other, ep)
    send_rest = remote(mine, x0t_ref.at[:, my_pos, :], misc_send.at[2], misc_recv.at[2], other, ep)
    y_copies = [remote(sources[n], places[n](ep), y_send.at[n], y_recv.at[n], other, ep) for n in pieces]
    x_copies = [remote(places[n](ep), places[n](ep), x_send.at[n], x_recv.at[n], tp, ep2) for n in pieces]
    c_copies = [remote(places[n](ep), places[n](ep), c_send.at[n], c_recv.at[n], tp, ep1) for n in pieces]
    d_copies = [remote(places[n](ep2), places[n](ep2), d_send.at[n], d_recv.at[n], tp, ep1) for n in pieces]
    send_u.start()
    for copy in y_copies[:4] + entry_copies + y_copies[4:] + [send_rest]:
        copy.start()

    def pass_on(n):
        arrived(places[n](ep), y_recv.at[n])
        x_copies[n].start()
        c_copies[n].start()

    def pass_across(n):
        arrived(places[n](ep2), x_recv.at[n])
        d_copies[n].start()

    def complete(n):
        arrived(places[n](ep1), c_recv.at[n])
        arrived(places[n](ep3), d_recv.at[n])

    def build_bias(rows_ref, side):
        u_rows[...] = bias_rows(rows_ref[...].reshape(u_rows.shape[0], rows_ref.shape[2]), seq_len)

        @pl.loop(0, 8)
        def _(n):
            layer, pair = n // 4, lax.rem(n, 4)
            for sub in range(2):
                row = u_rows[pl.ds(n * 2 + sub, 1), :]
                wide = pltpu.roll(jnp.broadcast_to(row, (seq_len, 2 * seq_len)), 0, 1, stride=1, stride_axis=0)
                at = slice(sub * half, (sub + 1) * half)
                place = layer * 8 + side * 4 + pair
                bias_low[place, at, :] = wide[:half, :half]
                bias_high[place, at, :] = wide[half:, :seq_len]

    def begin_seq(layer, s):
        rows = part(seq_len, s)
        a_ref[rows, :] = rms_rows(x[s], ln_attn_ref[layer])
        acc[rows, :] = x[s].astype(F32)

    def end_seq(s):
        x[s] = acc[part(seq_len, s), :].astype(BF16)

    def each_seq(step, *args):
        @pl.loop(0, seqs)
        def _(s):
            step(*args, s)

    first = lax.broadcasted_iota(jnp.int32, (1, 128), 1) < 64

    def products(layer, side, block, rows):
        for kind in range(3):
            qkv[kind, rows, :] = mm(a_ref[rows, :], w[layer, side, kind, :, block * quad:(block + 1) * quad]).astype(BF16)

    def attend_seq(layer, side, block, s):
        rows = part(seq_len, s)
        for pair in range(quad // 128):
            lanes = slice(pair * 128, (pair + 1) * 128)
            place = layer * 8 + side * 4 + block * (quad // 128) + pair
            q, k, v = (qkv[kind, rows, lanes] for kind in range(3))
            none = jnp.zeros_like(q[:half])
            outs = []
            for upper in range(2):
                qs = q[half:] if upper else q[:half]
                ks, vs = (k, v) if upper else (k[:half], v[:half])
                both = jnp.concatenate([jnp.where(first, qs, none), jnp.where(first, none, qs)], axis=0)
                bias = bias_high[place] if upper else bias_low[place]
                got = mm(softmax_bf16(mm_t(both, ks) * 0.125 + bias), vs)
                outs.append(jnp.where(first, got[:half], got[half:]))
            ctx[rows, lanes] = jnp.concatenate(outs, axis=0).astype(BF16)

    def project_seq(layer, side, block, s):
        rows = part(seq_len, s)
        acc[rows, :] += mm(ctx[rows, :], wo[layer, side, block * quad:(block + 1) * quad, :])

    def attend(layer, side, block):
        products(layer, side, block, slice(None))
        each_seq(attend_seq, layer, side, block)

    def project(layer, side, block):
        each_seq(project_seq, layer, side, block)

    def dense(s):
        h = x[s]
        b = rms_rows(h, ln_ffn_ref[0])
        total = h.astype(F32)
        for side in range(2):
            hid = (jax.nn.gelu(mm(b, gu[side, 0])) * mm(b, gu[side, 1])).astype(BF16)
            total = total + mm(hid, wd[side])
        x[s] = total.astype(BF16)

    def heads(layer, side, block):
        attend(layer, side, block)
        project(layer, side, block)

    build_bias(table_ref, 0)
    arrived(table_other, misc_recv.at[1])
    build_bias(table_other, 1)
    own_stage.wait()
    own_x0t = pltpu.make_async_copy(stage, x0t_ref.at[:, my_pos, :], out_sem.at[0])
    own_x0t.start()

    with scope("w_l0_y"):
        for n in range(4):
            pass_on(n)
    with scope("w_l0_x"):
        for n in range(4):
            pass_across(n)
    own_x.wait()
    for n in range(4):
        own_loads[n].wait()
        complete(n)

    def x0_copy(s):
        return pltpu.make_async_copy(x.at[s], x0_ref.at[s], x0_sem.at[s])

    @pl.loop(0, seqs)
    def _(s):
        with scope("w_entry"):
            arrived(x.at[s, part(half, other), :], entry_recv.at[s])
        x0_copy(s).start()
        begin_seq(0, s)
        for side in range(2):
            for block in range(2):
                products(0, side, block, part(seq_len, s))
                attend_seq(0, side, block, s)
                project_seq(0, side, block, s)
        x0_copy(s).wait()
        end_seq(s)

        @pl.when(s == seqs - 2)
        def _():
            pass_on(4)

    with scope("w_ffn_y"):
        for n in range(5, 7):
            pass_on(n)
        pass_on(7)
    with scope("w_ffn_x"):
        for n in range(4, 7):
            pass_across(n)
    with scope("w_ffn_all"):
        for n in range(4, 7):
            own_loads[n].wait()
            complete(n)

    @pl.loop(0, seqs // 2)
    def _(s):
        dense(s)

    with scope("w_l1_k"):
        pass_on(8)

    @pl.loop(seqs // 2, seqs)
    def _(s):
        dense(s)

    out_h1 = pltpu.make_async_copy(x, h1_ref, out_sem.at[2])
    out_h1.start()
    each_seq(begin_seq, 1)
    for n in range(7, 11):
        own_loads[n].wait()
    attend(1, 0, 0)
    with scope("w_l1_v"):
        pass_on(9)
    project(1, 0, 0)
    heads(1, 0, 1)
    with scope("w_l1_o"):
        pass_on(10)
    with scope("w_l1_x"):
        for n in range(7, 10):
            pass_across(n)
    with scope("w_l1_all"):
        for n in range(7, 10):
            complete(n)
    attend(1, 1, 0)
    with scope("w_l1_o_all"):
        pass_across(10)
        complete(10)
    project(1, 1, 0)
    heads(1, 1, 1)
    out_h1.wait()
    each_seq(end_seq)
    out_h2 = pltpu.make_async_copy(x, h2_ref, out_sem.at[3])
    out_h2.start()

    with scope("w_rest"):
        arrived(x0t_ref.at[:, part(half, other), :], misc_recv.at[2])
    own_x0t.wait()
    for copy in entry_copies + [send_u, send_rest] + y_copies + x_copies + c_copies + d_copies:
        copy.wait_send()
    out_h2.wait()


def dense_layers(hidden_in, ln_attn, ln_ffn, w_query, w_key, w_value, w_out, bias_table, w_gate, w_up, w_down):
    batch, positions, d_model = hidden_in.shape
    seqs, seq_len = batch // 2, 2 * positions
    inner = w_query.shape[2]
    any_spec = pl.BlockSpec(memory_space=pl.ANY)
    vmem_spec = pl.BlockSpec(memory_space=pltpu.VMEM)
    dma = pltpu.SemaphoreType.DMA
    shape = jax.ShapeDtypeStruct((seqs, seq_len, d_model), BF16)
    return pl.pallas_call(
        layers_body,
        in_specs=[any_spec, vmem_spec, vmem_spec] + [any_spec] * 4 + [vmem_spec] + [any_spec] * 3,
        out_specs=[any_spec] * 4,
        out_shape=[shape] * 4,
        scratch_shapes=[
            pltpu.VMEM(shape.shape, BF16),
            pltpu.VMEM((seqs * seq_len, d_model), BF16),
            pltpu.VMEM((seqs * seq_len, d_model), F32),
            pltpu.VMEM((2, 2, 3, d_model, inner), BF16),
            pltpu.VMEM((2, 2, inner, d_model), BF16),
            pltpu.VMEM((2, 2) + w_gate.shape, BF16),
            pltpu.VMEM((2,) + w_down.shape, BF16),
            pltpu.VMEM(bias_table.shape, F32),
            pltpu.VMEM((bias_table.shape[0] * bias_table.shape[1], 2 * seq_len), F32),
            pltpu.VMEM((16, seq_len, seq_len // 2), F32),
            pltpu.VMEM((16, seq_len, seq_len), F32),
            pltpu.VMEM((3, seqs * seq_len, 256), BF16),
            pltpu.VMEM((seqs * seq_len, 256), BF16),
            pltpu.VMEM((seqs, positions, d_model), BF16),
            dma((2,)), dma((11,)), dma((4,)), dma((seqs,)), dma((seqs,)), dma((seqs,)), dma((3,)), dma((3,)),
        ] + [dma((11,))] * 8,
        compiler_params=pltpu.CompilerParams(vmem_limit_bytes=VMEM_LIMIT, collective_id=1, has_side_effects=True),
        cost_estimate=pl.CostEstimate(flops=32_000_000_000, bytes_accessed=40 << 20, transcendentals=0),
        name="dense_layers",
    )(hidden_in, ln_attn, ln_ffn, w_query, w_key, w_value, w_out, bias_table, w_gate, w_up, w_down)


def moe_body(h2_ref, h1_ref, x0_ref, x0t_ref, ids_ref, ln_ffn_ref, ln_attn_ref, router_ref,
             w_in_hbm, w_out_hbm, wk_hbm, wv_hbm,
             out_ref, k_ref, v_ref, h1t_ref,
             hall, res, ret, w_in, w_out, wkv, acc, slot_row_ref, slots_all, columns_ref, gates, xbuf, kvbuf,
             in_sem, cache_sem, store_sem, slot_send, slot_recv, hs_send, hs_recv, ret_send, ret_recv, h1_send, h1_recv):
    tp, ep = lax.axis_index('tp'), lax.axis_index('ep')
    other = 1 - tp
    ep1, ep2, ep3 = axis_neighbours(tp, ep)
    me = tp * 4 + ep
    seqs, seq_len, d_model = h2_ref.shape
    tokens = acc.shape[0]
    rows = res.shape[1]
    half_pos = seq_len // 2
    experts = w_in.shape[0]
    capacity = rows // experts

    loads = [pltpu.make_async_copy(a, b, in_sem.at[n]) for n, (a, b) in enumerate((
        (x0_ref, xbuf), (wk_hbm, wkv.at[0]), (wv_hbm, wkv.at[1]), (h2_ref, hall.at[me]),
        (w_in_hbm, w_in), (w_out_hbm, w_out)))]
    for load in loads:
        load.start()

    barrier = pltpu.get_barrier_semaphore()
    peers = [(other, ep), (tp, ep2), (tp, ep1), (other, ep1), (other, ep2), (tp, ep3), (other, ep3)]
    for peer_tp, peer_ep in peers:
        pl.semaphore_signal(barrier, inc=1, device_id=(lax.axis_index('dp'), peer_tp, peer_ep), device_id_type=MESH)
    pl.semaphore_wait(barrier, len(peers))

    def half_at(k):
        return pl.ds(pl.multiple_of(k * half_pos, half_pos), half_pos)

    def block(owner, k):
        return hall.at[owner, :, half_at(k), :]

    sends = []
    for n, peer in enumerate(((other, ep), (tp, ep2), (tp, ep1))):
        for k in ((other, tp) if n == 0 else (tp, other)):
            sends.append(remote(h2_ref.at[:, half_at(k), :], block(me, k), hs_send.at[n, k], hs_recv.at[me, k], *peer))
    for copy in sends:
        copy.start()

    def arrived(ref, sem):
        remote(ref, ref, hs_send.at[0], sem, tp, ep).wait_recv()

    def block_arrived(owner, k):
        arrived(block(owner, k), hs_recv.at[owner, k])

    def forward(n, owner, k, *peer):
        copy = remote(block(owner, k), block(owner, k), hs_send.at[n, k], hs_recv.at[owner, k], *peer)
        copy.start()
        sends.append(copy)

    num_experts = router_ref.shape[0]
    ids_row = jnp.concatenate([ids_ref[s] for s in range(ids_ref.shape[0])], axis=1)
    expert = lax.broadcasted_iota(jnp.int32, (num_experts, tokens), 0)
    hot = [jnp.where(ids_row[c:c + 1] == expert, 1.0, 0.0) for c in range(2)]
    earlier = lax.broadcasted_iota(jnp.int32, (tokens, tokens), 0) <= lax.broadcasted_iota(jnp.int32, (tokens, tokens), 1)
    upto = mm(jnp.concatenate(hot, axis=0).astype(BF16), jnp.where(earlier, 1.0, 0.0).astype(BF16))
    base = (0.0, upto[:num_experts, tokens - 1:])
    wide_ids = ids_row.astype(F32)
    slot_rows = []
    for c in range(2):
        place = jnp.sum((upto[c * num_experts:(c + 1) * num_experts] - 1.0 + base[c]) * hot[c], axis=0, keepdims=True)
        slot_rows.append(jnp.where(place < capacity, wide_ids[c:c + 1] * capacity + place, -1.0))
    packed = jnp.concatenate(slot_rows + [wide_ids, jnp.zeros((4, tokens), F32)], axis=0)
    slot_row_ref[...] = packed[:2].astype(jnp.int32)
    slots_all[me] = packed[:2].astype(jnp.int32)
    columns_ref[...] = packed.T.astype(jnp.int32)
    slot_copies = [remote(slot_row_ref, slots_all.at[me], slot_send.at[n], slot_recv.at[me], *peer) for n, peer in enumerate(peers)]
    for copy in slot_copies:
        copy.start()
    send_h1 = remote(h1_ref, h1t_ref, h1_send, h1_recv, other, ep)
    send_h1.start()

    def cache_part(source, layer, owner, load=None):
        if load is None:
            load = pltpu.make_async_copy(source, xbuf, cache_sem)
            load.start()
        load.wait()

        @pl.loop(0, seqs)
        def _(s):
            a = rms_rows(xbuf[s], ln_attn_ref[layer])
            for n, ref in enumerate((k_ref, v_ref)):
                full = mm(a, wkv[n, layer])
                kvbuf[s, n] = full.T.astype(BF16).reshape(kvbuf.shape[2:])
                pltpu.make_async_copy(kvbuf.at[s, n], ref.at[layer, owner * seqs + s], store_sem.at[s, n]).start()

        @pl.loop(0, seqs)
        def _(s):
            for n, ref in enumerate((k_ref, v_ref)):
                pltpu.make_async_copy(kvbuf.at[s, n], ref.at[layer, owner * seqs + s], store_sem.at[s, n]).wait()

    loads[1].wait()
    loads[2].wait()
    cache_part(x0_ref, 0, tp, loads[0])
    cache_part(x0t_ref, 0, other)
    cache_part(h1_ref, 1, tp)

    y_owner, x_owner, c_owner = other * 4 + ep, tp * 4 + ep2, tp * 4 + ep1
    yx_owner, yc_owner, xc_owner, yxc_owner = other * 4 + ep2, other * 4 + ep1, tp * 4 + ep3, other * 4 + ep3
    for place, k in enumerate((tp, other)):
        with scope(f"w_y{place}"):
            block_arrived(y_owner, k)
        forward(3, y_owner, k, tp, ep2)
        forward(4, y_owner, k, tp, ep1)
    loads[3].wait()

    def own_tokens(owner):
        return hall[owner, :, half_at(tp), :].reshape(tokens // 2, d_model)

    for part in range(2):
        at = slice(part * (tokens // 2), (part + 1) * (tokens // 2))
        h_own = own_tokens(part * 4 + ep)
        acc[at] = h_own.astype(F32)
        b = rms_rows(h_own, ln_ffn_ref[1])
        logits = lax.dot_general(b.astype(F32), router_ref[...], (((1,), (1,)), ((), ())),
                                 precision=lax.Precision.HIGHEST, preferred_element_type=F32)
        grown = jnp.exp(logits - jnp.max(logits, axis=-1, keepdims=True))
        probs = grown / jnp.sum(grown, axis=-1, keepdims=True)
        lanes = lax.broadcasted_iota(jnp.int32, probs.shape, 1)
        picked = [jnp.sum(jnp.where(columns_ref[at, 2 + c:3 + c] == lanes, probs, 0.0), axis=-1, keepdims=True) for c in range(2)]
        both = picked[0] + picked[1]
        gates[at, 0:1] = picked[0] / both
        gates[at, 1:2] = picked[1] / both

    with scope("w_x"):
        for k in (tp, other):
            block_arrived(x_owner, k)
            forward(5, x_owner, k, tp, ep1)
    for peer_tp, peer_ep in peers:
        arrived(slots_all.at[peer_tp * 4 + peer_ep], slot_recv.at[peer_tp * 4 + peer_ep])
    loads[4].wait()
    loads[5].wait()

    def run_group(i, k):
        dest = k * 4 + i
        slots = slots_all[dest]
        want = me * rows + lax.broadcasted_iota(jnp.int32, (rows, tokens // 2), 0)
        chosen = None
        for part in range(2):
            h = hall[part * 4 + i, :, half_at(k), :].reshape(tokens // 2, d_model)
            at = slice(part * (tokens // 2), (part + 1) * (tokens // 2))
            pick = jnp.logical_or(slots[0:1, at] == want, slots[1:2, at] == want)
            term = mm(jnp.where(pick, 1.0, 0.0).astype(BF16), h)
            chosen = term if chosen is None else chosen + term
        b = rms_rows(chosen, ln_ffn_ref[1])
        for e in range(experts):
            at = slice(e * capacity, (e + 1) * capacity)
            hid = jax.nn.gelu(mm(b[at], w_in[e])).astype(BF16)
            res[dest, at] = mm(hid, w_out[e]).astype(BF16)
        return dest

    def give_back(i, k):
        dest = k * 4 + i
        return remote(res.at[dest], ret.at[me], ret_send.at[dest], ret_recv.at[me], k, i)

    def add_rows(source_ref, owner):
        step = 256

        @pl.loop(0, tokens // step)
        def _(r):
            at = pl.ds(pl.multiple_of(r * step, step), step)
            columns = owner * rows + lax.broadcasted_iota(jnp.int32, (step, rows), 1)
            total = acc[at, :]
            for c in range(2):
                pick = jnp.where(columns_ref[at, c:c + 1] == columns, 1.0, 0.0).astype(BF16)
                total = total + gates[at, c:c + 1] * mm(pick, source_ref[...])
            acc[at, :] = total

    with scope("w_yc"):
        for k in range(2):
            block_arrived(c_owner, k)
            block_arrived(yc_owner, k)

    @pl.loop(0, 4)
    def _(t):
        late = t // 2
        beside = lax.rem((t + 1) // 2, 2)
        i = ep + beside * (ep1 - ep)
        k = late * tp + (1 - late) * other
        run_group(i, k)

        @pl.when(t < 3)
        def _():
            give_back(i, k).start()

    add_rows(res.at[me], me)

    for place, k in enumerate((tp, other)):
        with scope(f"w_yx{place}"):
            block_arrived(yx_owner, k)
        forward(6, yx_owner, k, tp, ep1)
        with scope(f"w_far{place}"):
            block_arrived(xc_owner, k)
            block_arrived(yxc_owner, k)

        @pl.loop(0, 2)
        def _(t):
            i = (1 - t) * ep2 + t * ep3
            run_group(i, k)
            give_back(i, k).start()

        if place == 0:
            with scope("w_h1"):
                arrived(h1t_ref, h1_recv)
            cache_part(h1t_ref, 1, other)

    @pl.loop(1, 8)
    def _(n):
        across, beside, far = lax.rem(n // 2, 2), lax.rem(n, 2), n // 4
        peer_tp = tp + across * (other - tp)
        peer_ep = lax.rem(ep + beside * (ep1 - ep) + 2 * far, 4)
        owner = peer_tp * 4 + peer_ep
        with scope("w_ret"):
            arrived(ret.at[owner], ret_recv.at[owner])
        add_rows(ret.at[owner], owner)

    out_ref[...] = acc[...].astype(BF16)

    for copy in sends + slot_copies + [send_h1]:
        copy.wait_send()
    for peer_tp, peer_ep in peers:
        give_back(peer_ep, peer_tp).wait_send()


def moe_layer(h2, h1, x0, x0t, expert_ids, ln_ffn, ln_attn, w_router, expert_in, expert_out, w_key, w_value):
    seqs, seq_len, d_model = h2.shape
    tokens = seqs * seq_len
    experts, _, d_ff = expert_in.shape
    groups = 8
    rows = experts * 4 * tokens // (experts * groups)
    inner = w_key.shape[2]
    heads = inner // 64
    any_spec = pl.BlockSpec(memory_space=pl.ANY)
    vmem_spec = pl.BlockSpec(memory_space=pltpu.VMEM)
    cache_shape = jax.ShapeDtypeStruct((2, 2 * seqs, heads, 64, seq_len), BF16)
    dma = pltpu.SemaphoreType.DMA
    return pl.pallas_call(
        moe_body,
        in_specs=[any_spec] * 4 + [vmem_spec] * 4 + [any_spec] * 4,
        out_specs=[vmem_spec, any_spec, any_spec, any_spec],
        out_shape=[jax.ShapeDtypeStruct((tokens, d_model), BF16), cache_shape, cache_shape, jax.ShapeDtypeStruct(h1.shape, BF16)],
        scratch_shapes=[
            pltpu.VMEM((groups,) + h2.shape, BF16),
            pltpu.VMEM((groups, rows, d_model), BF16),
            pltpu.VMEM((groups, rows, d_model), BF16),
            pltpu.VMEM(expert_in.shape, BF16),
            pltpu.VMEM(expert_out.shape, BF16),
            pltpu.VMEM((2, 2, d_model, inner), BF16),
            pltpu.VMEM((tokens, d_model), F32),
            pltpu.VMEM((2, tokens), jnp.int32),
            pltpu.VMEM((groups, 2, tokens), jnp.int32),
            pltpu.VMEM((tokens, 8), jnp.int32),
            pltpu.VMEM((tokens, 2), F32),
            pltpu.VMEM(h1.shape, BF16),
            pltpu.VMEM((seqs, 2, heads, 64, seq_len), BF16),
            dma((6,)), dma, dma((seqs, 2)), dma((7,)), dma((groups,)), dma((7, 2)), dma((groups, 2)),
            dma((groups,)), dma((groups,)), dma, dma,
        ],
        compiler_params=pltpu.CompilerParams(vmem_limit_bytes=67043328, collective_id=2, has_side_effects=True),
        cost_estimate=pl.CostEstimate(flops=40_000_000_000, bytes_accessed=64 << 20, transcendentals=0),
        name="moe",
    )(h2, h1, x0, x0t, jnp.swapaxes(expert_ids, 1, 2), ln_ffn, ln_attn, w_router.T, expert_in, expert_out, w_key, w_value)


def solution(mesh):
    act_spec = P(('dp', 'ep'), 'tp', None)
    col_spec = P(None, None, 'tp')
    row_spec = P(None, 'tp', None)
    expert_spec = P(('tp', 'ep'), None, None)
    cache_spec = P(None, ('dp', 'ep'), 'tp', None, None)
    in_specs = (act_spec, P(), P(), col_spec, col_spec, col_spec, row_spec, row_spec,
                P(None, 'tp'), P(None, 'tp'), P('tp', None), P(), expert_spec, expert_spec, act_spec)

    def device_fn(hidden_in, ln_attn, ln_ffn, w_query, w_key, w_value, w_out, bias_table, w_gate, w_up, w_down, w_router, expert_in, expert_out, expert_ids):
        h1, h2, x0, x0t = dense_layers(hidden_in, ln_attn, ln_ffn, w_query, w_key, w_value, w_out, bias_table, w_gate, w_up, w_down)
        hidden, k_cache, v_cache, _ = moe_layer(
            h2, h1, x0, x0t, expert_ids, ln_ffn, ln_attn, w_router, expert_in, expert_out, w_key, w_value)
        return hidden.reshape(hidden_in.shape), jnp.swapaxes(k_cache, 3, 4), jnp.swapaxes(v_cache, 3, 4)

    return jax.shard_map(device_fn, mesh=mesh, in_specs=in_specs, out_specs=(act_spec, cache_spec, cache_spec), check_vma=False)
```

profile of v0, /device:TPU:0, one launch (start us, length us, event | category | flops | bytes accessed | tf_op | source)
XLA Modules:
  0.0 314.7 jit_solution(13548983047502666130)
XLA Ops:
  0.6 114.9 %dense_layers.1 = (bf16[4,256,1024]{2,1,0:T(8,128)(2,1)}, bf16[4,256,1024]{2,1,0:T(8,128)(2,1)}, bf16[4,256,1024]{2,1,0:T(8,128)(2,1)}, bf16[4,256,1024]{2,1,0:T(8,128)(2,1)}) custom-call(bf16[8,128,1024]{2,1,0:T(8,128)(2,1)} %hid_ref.1, f32[2,1024]{1,0:T(2,128)} %ln_attn_ref.3, f32[2,1024]{1,0:T(2,128)} %ln_ffn_ref.3, bf16[2,1024,512]{2,1,0:T(8,128)(2,1)} %wq_hbm.1, ...), custom_call_target="tpu_custom_call" | custom-call | flops 32000000000 | bytes 41943040 | tf_op jit(solution)/shard_map/dense_layers/pallas_call | solution.py:328
  115.5 190.2 %moe.1 = (bf16[1024,1024]{1,0:T(8,128)(2,1)}, bf16[2,8,8,64,256]{4,3,2,1,0:T(8,128)(2,1)}, bf16[2,8,8,64,256]{4,3,2,1,0:T(8,128)(2,1)}, bf16[4,256,1024]{2,1,0:T(8,128)(2,1)}) custom-call(bf16[4,256,1024]{2,1,0:T(8,128)(2,1)} %get-tuple-element.10.h2_ref, bf16[4,256,1024]{2,1,0:T(8,128)(2,1)} %get-tuple-element.11.h1_ref, ...), custom_call_target="tpu_custom_call" | custom-call | flops 40000000000 | bytes 67108864 | tf_op jit(solution)/shard_map/moe/pallas_call | solution.py:594
  305.7 0.0 copy-start.1
  305.7 3.2 %copy.21 = bf16[8,128,1024]{2,1,0:T(8,128)(2,1)} copy(bf16[8,128,1024]{2,1,0:T(8,128)(2,1)} %bitcast.7) | data formatting | bytes 4194304
  308.9 0.0 copy-done.1
  308.9 0.0 copy-start
  308.9 2.1 copy.22
  311.1 1.6 copy-done
  312.6 2.0 copy.23
Async XLA Ops:
  305.7 3.3 %copy-start.1 = (bf16[2,8,8,64,256]{4,3,2,1,0:T(8,128)(2,1)S(1)}, bf16[2,8,8,64,256]{4,3,2,1,0:T(8,128)(2,1)}, u32[]{:S(2)}) copy-start(bf16[2,8,8,64,256]{4,3,2,1,0:T(8,128)(2,1)} %get-tuple-element.15) | copy-start | bytes 12582916
  308.9 3.7 %copy-start = (bf16[2,8,8,64,256]{4,3,2,1,0:T(8,128)(2,1)S(1)}, bf16[2,8,8,64,256]{4,3,2,1,0:T(8,128)(2,1)}, u32[]{:S(2)}) copy-start(bf16[2,8,8,64,256]{4,3,2,1,0:T(8,128)(2,1)} %get-tuple-element.16) | copy-start | bytes 12582916
where the time goes:
time: 315 us
  Pallas kernels  305 us (97%)
  local copies, waits for them, and re-layouts  8.96 us (3%)
    pallas_call x1, Pallas kernels, moe_layer(): pl.pallas_call(moe_body, in_specs=[any_spec] * 4 + [vmem_spec] * 4 + [any...  190 us
    pallas_call x1, Pallas kernels, dense_layers(): pl.pallas_call(layers_body, in_specs=[any_spec, vmem_spec, vmem_spec] + [...  115 us
    unnamed x7, local copies, waits for them, and re-layouts  8.96 us

commit v1 on v0

--- a/solution.py
+++ b/solution.py
@@ -250,6 +250,11 @@
                 products(0, side, block, part(seq_len, s))
                 attend_seq(0, side, block, s)
                 project_seq(0, side, block, s)
+            if side == 0:
+                @pl.when(s == seqs - 1)
+                def _():
+                    pass_on(5)
+                    pass_on(6)
         x0_copy(s).wait()
         end_seq(s)
 
@@ -258,8 +263,6 @@
             pass_on(4)
 
     with scope("w_ffn_y"):
-        for n in range(5, 7):
-            pass_on(n)
         pass_on(7)
     with scope("w_ffn_x"):
         for n in range(4, 7):
@@ -506,17 +509,20 @@
             res[dest, at] = mm(hid, w_out[e]).astype(BF16)
         return dest
 
+    some = rows // 2
+
     def give_back(i, k):
         dest = k * 4 + i
-        return remote(res.at[dest], ret.at[me], ret_send.at[dest], ret_recv.at[me], k, i)
-
-    def add_rows(source_ref, owner):
+        return [remote(res.at[dest, pl.ds(p * some, some), :], ret.at[me, pl.ds(p * some, some), :],
+                       ret_send.at[dest, p], ret_recv.at[me, p], k, i) for p in range(2)]
+
+    def add_rows(source_ref, base, rows):
         step = 256
 
         @pl.loop(0, tokens // step)
         def _(r):
             at = pl.ds(pl.multiple_of(r * step, step), step)
-            columns = owner * rows + lax.broadcasted_iota(jnp.int32, (step, rows), 1)
+            columns = base + lax.broadcasted_iota(jnp.int32, (step, rows), 1)
             total = acc[at, :]
             for c in range(2):
                 pick = jnp.where(columns_ref[at, c:c + 1] == columns, 1.0, 0.0).astype(BF16)
@@ -538,9 +544,10 @@
 
         @pl.when(t < 3)
         def _():
-            give_back(i, k).start()
-
-    add_rows(res.at[me], me)
+            for copy in give_back(i, k):
+                copy.start()
+
+    add_rows(res.at[me], me * rows, rows)
 
     for place, k in enumerate((tp, other)):
         with scope(f"w_yx{place}"):
@@ -554,7 +561,8 @@
         def _(t):
             i = (1 - t) * ep2 + t * ep3
             run_group(i, k)
-            give_back(i, k).start()
+            for copy in give_back(i, k):
+                copy.start()
 
         if place == 0:
             with scope("w_h1"):
@@ -567,16 +575,17 @@
         peer_tp = tp + across * (other - tp)
         peer_ep = lax.rem(ep + beside * (ep1 - ep) + 2 * far, 4)
         owner = peer_tp * 4 + peer_ep
-        with scope("w_ret"):
-            arrived(ret.at[owner], ret_recv.at[owner])
-        add_rows(ret.at[owner], owner)
+        for p in range(2):
+            arrived(ret.at[owner, pl.ds(p * some, some), :], ret_recv.at[owner, p])
+            add_rows(ret.at[owner, pl.ds(p * some, some), :], owner * rows + p * some, some)
 
     out_ref[...] = acc[...].astype(BF16)
 
     for copy in sends + slot_copies + [send_h1]:
         copy.wait_send()
     for peer_tp, peer_ep in peers:
-        give_back(peer_ep, peer_tp).wait_send()
+        for copy in give_back(peer_ep, peer_tp):
+            copy.wait_send()
 
 
 def moe_layer(h2, h1, x0, x0t, expert_ids, ln_ffn, ln_attn, w_router, expert_in, expert_out, w_key, w_value):
@@ -611,7 +620,7 @@
             pltpu.VMEM(h1.shape, BF16),
             pltpu.VMEM((seqs, 2, heads, 64, seq_len), BF16),
             dma((6,)), dma, dma((seqs, 2)), dma((7,)), dma((groups,)), dma((7, 2)), dma((groups, 2)),
-            dma((groups,)), dma((groups,)), dma, dma,
+            dma((groups, 2)), dma((groups, 2)), dma, dma,
         ],
         compiler_params=pltpu.CompilerParams(vmem_limit_bytes=67043328, collective_id=2, has_side_effects=True),
         cost_estimate=pl.CostEstimate(flops=40_000_000_000, bytes_accessed=64 << 20, transcendentals=0),

time: 315 us -> 311 us (0.987)
  Pallas kernels: 305 us -> 301 us
    pallas_call x1, Pallas kernels: 115 us -> 112 us  [dense_layers(): pl.pallas_call(layers_body, in_specs=[any_spec, vmem_spec, vmem_spec] + [...]
where the time goes in v1:
time: 311 us; the launch traced here: 310 us
  Pallas kernels  301 us (97%)
  local copies, waits for them, and re-layouts  8.96 us (3%)
    pallas_call x1, Pallas kernels, moe_layer(): pl.pallas_call(moe_body, in_specs=[any_spec] * 4 + [vmem_spec] * 4 + [any...  189 us
    pallas_call x1, Pallas kernels, dense_layers(): pl.pallas_call(layers_body, in_specs=[any_spec, vmem_spec, vmem_spec] + [...  112 us
    unnamed x7, local copies, waits for them, and re-layouts  8.96 us

profile of v1, /device:TPU:0, one launch (start us, length us, event | category | flops | bytes accessed | tf_op | source)
XLA Modules:
  0.0 310.4 jit_solution(13303497920266484184)
XLA Ops:
  0.6 111.5 %dense_layers.1 = (bf16[4,256,1024]{2,1,0:T(8,128)(2,1)}, bf16[4,256,1024]{2,1,0:T(8,128)(2,1)}, bf16[4,256,1024]{2,1,0:T(8,128)(2,1)}, bf16[4,256,1024]{2,1,0:T(8,128)(2,1)}) custom-call(bf16[8,128,1024]{2,1,0:T(8,128)(2,1)} %hid_ref.1, f32[2,1024]{1,0:T(2,128)} %ln_attn_ref.3, f32[2,1024]{1,0:T(2,128)} %ln_ffn_ref.3, bf16[2,1024,512]{2,1,0:T(8,128)(2,1)} %wq_hbm.1, ...), custom_call_target="tpu_custom_call" | custom-call | flops 32000000000 | bytes 41943040 | tf_op jit(solution)/shard_map/dense_layers/pallas_call | solution.py:331
  112.2 189.3 %moe.1 = (bf16[1024,1024]{1,0:T(8,128)(2,1)}, bf16[2,8,8,64,256]{4,3,2,1,0:T(8,128)(2,1)}, bf16[2,8,8,64,256]{4,3,2,1,0:T(8,128)(2,1)}, bf16[4,256,1024]{2,1,0:T(8,128)(2,1)}) custom-call(bf16[4,256,1024]{2,1,0:T(8,128)(2,1)} %get-tuple-element.10.h2_ref, bf16[4,256,1024]{2,1,0:T(8,128)(2,1)} %get-tuple-element.11.h1_ref, ...), custom_call_target="tpu_custom_call" | custom-call | flops 40000000000 | bytes 67108864 | tf_op jit(solution)/shard_map/moe/pallas_call | solution.py:603
  301.4 0.0 copy-start.1
  301.4 3.2 %copy.21 = bf16[8,128,1024]{2,1,0:T(8,128)(2,1)} copy(bf16[8,128,1024]{2,1,0:T(8,128)(2,1)} %bitcast.7) | data formatting | bytes 4194304
  304.7 0.0 copy-done.1
  304.7 0.0 copy-start
  304.7 2.1 copy.22
  306.8 1.6 copy-done
  308.4 2.0 copy.23
Async XLA Ops:
  301.4 3.3 %copy-start.1 = (bf16[2,8,8,64,256]{4,3,2,1,0:T(8,128)(2,1)S(1)}, bf16[2,8,8,64,256]{4,3,2,1,0:T(8,128)(2,1)}, u32[]{:S(2)}) copy-start(bf16[2,8,8,64,256]{4,3,2,1,0:T(8,128)(2,1)} %get-tuple-element.15) | copy-start | bytes 12582916
  304.7 3.7 %copy-start = (bf16[2,8,8,64,256]{4,3,2,1,0:T(8,128)(2,1)S(1)}, bf16[2,8,8,64,256]{4,3,2,1,0:T(8,128)(2,1)}, u32[]{:S(2)}) copy-start(bf16[2,8,8,64,256]{4,3,2,1,0:T(8,128)(2,1)} %get-tuple-element.16) | copy-start | bytes 12582916

commit v2 on v1

--- a/solution.py
+++ b/solution.py
@@ -516,8 +516,11 @@
         return [remote(res.at[dest, pl.ds(p * some, some), :], ret.at[me, pl.ds(p * some, some), :],
                        ret_send.at[dest, p], ret_recv.at[me, p], k, i) for p in range(2)]
 
-    def add_rows(source_ref, base, rows):
-        step = 256
+    def out_copy(r):
+        return pltpu.make_async_copy(xbuf.at[r], out_ref.at[pl.ds(r * seq_len, seq_len), :], in_sem.at[r])
+
+    def add_rows(source_ref, base, rows, last=None):
+        step = seq_len
 
         @pl.loop(0, tokens // step)
         def _(r):
@@ -528,6 +531,11 @@
                 pick = jnp.where(columns_ref[at, c:c + 1] == columns, 1.0, 0.0).astype(BF16)
                 total = total + gates[at, c:c + 1] * mm(pick, source_ref[...])
             acc[at, :] = total
+            if last is not None:
+                @pl.when(last)
+                def _():
+                    xbuf[r] = total.astype(BF16)
+                    out_copy(r).start()
 
     with scope("w_yc"):
         for k in range(2):
@@ -577,9 +585,10 @@
         owner = peer_tp * 4 + peer_ep
         for p in range(2):
             arrived(ret.at[owner, pl.ds(p * some, some), :], ret_recv.at[owner, p])
-            add_rows(ret.at[owner, pl.ds(p * some, some), :], owner * rows + p * some, some)
-
-    out_ref[...] = acc[...].astype(BF16)
+            add_rows(ret.at[owner, pl.ds(p * some, some), :], owner * rows + p * some, some, n == 7 if p == 1 else None)
+
+    for r in range(seqs):
+        out_copy(r).wait()
 
     for copy in sends + slot_copies + [send_h1]:
         copy.wait_send()
@@ -603,7 +612,7 @@
     return pl.pallas_call(
         moe_body,
         in_specs=[any_spec] * 4 + [vmem_spec] * 4 + [any_spec] * 4,
-        out_specs=[vmem_spec, any_spec, any_spec, any_spec],
+        out_specs=[any_spec] * 4,
         out_shape=[jax.ShapeDtypeStruct((tokens, d_model), BF16), cache_shape, cache_shape, jax.ShapeDtypeStruct(h1.shape, BF16)],
         scratch_shapes=[
             pltpu.VMEM((groups,) + h2.shape, BF16),

time: 311 us -> 310 us (level)
  no operation moved by 1% of the time
where the time goes in v2:
time: 310 us
  Pallas kernels  300 us (97%)
  local copies, waits for them, and re-layouts  8.96 us (3%)
    pallas_call x1, Pallas kernels, moe_layer(): pl.pallas_call(moe_body, in_specs=[any_spec] * 4 + [vmem_spec] * 4 + [any...  189 us
    pallas_call x1, Pallas kernels, dense_layers(): pl.pallas_call(layers_body, in_specs=[any_spec, vmem_spec, vmem_spec] + [...  112 us
    unnamed x7, local copies, waits for them, and re-layouts  8.96 us

profile of v2, /device:TPU:0, one launch (start us, length us, event | category | flops | bytes accessed | tf_op | source)
XLA Modules:
  0.0 309.9 jit_solution(13631292933336637102)
XLA Ops:
  0.6 111.5 %dense_layers.1 = (bf16[4,256,1024]{2,1,0:T(8,128)(2,1)}, bf16[4,256,1024]{2,1,0:T(8,128)(2,1)}, bf16[4,256,1024]{2,1,0:T(8,128)(2,1)}, bf16[4,256,1024]{2,1,0:T(8,128)(2,1)}) custom-call(bf16[8,128,1024]{2,1,0:T(8,128)(2,1)} %hid_ref.1, f32[2,1024]{1,0:T(2,128)} %ln_attn_ref.3, f32[2,1024]{1,0:T(2,128)} %ln_ffn_ref.3, bf16[2,1024,512]{2,1,0:T(8,128)(2,1)} %wq_hbm.1, ...), custom_call_target="tpu_custom_call" | custom-call | flops 32000000000 | bytes 41943040 | tf_op jit(solution)/shard_map/dense_layers/pallas_call | solution.py:331
  112.2 188.8 %moe.1 = (bf16[1024,1024]{1,0:T(8,128)(2,1)}, bf16[2,8,8,64,256]{4,3,2,1,0:T(8,128)(2,1)}, bf16[2,8,8,64,256]{4,3,2,1,0:T(8,128)(2,1)}, bf16[4,256,1024]{2,1,0:T(8,128)(2,1)}) custom-call(bf16[4,256,1024]{2,1,0:T(8,128)(2,1)} %get-tuple-element.10.h2_ref, bf16[4,256,1024]{2,1,0:T(8,128)(2,1)} %get-tuple-element.11.h1_ref, ...), custom_call_target="tpu_custom_call" | custom-call | flops 40000000000 | bytes 67108864 | tf_op jit(solution)/shard_map/moe/pallas_call | solution.py:612
  300.9 0.0 copy-start.1
  300.9 3.2 %copy.21 = bf16[8,128,1024]{2,1,0:T(8,128)(2,1)} copy(bf16[8,128,1024]{2,1,0:T(8,128)(2,1)} %bitcast.7) | data formatting | bytes 4194304
  304.2 0.0 copy-done.1
  304.2 0.0 copy-start
  304.2 2.1 copy.22
  306.3 1.6 copy-done
  307.9 2.0 copy.23
Async XLA Ops:
  300.9 3.3 %copy-start.1 = (bf16[2,8,8,64,256]{4,3,2,1,0:T(8,128)(2,1)S(1)}, bf16[2,8,8,64,256]{4,3,2,1,0:T(8,128)(2,1)}, u32[]{:S(2)}) copy-start(bf16[2,8,8,64,256]{4,3,2,1,0:T(8,128)(2,1)} %get-tuple-element.15) | copy-start | bytes 12582916
  304.2 3.7 %copy-start = (bf16[2,8,8,64,256]{4,3,2,1,0:T(8,128)(2,1)S(1)}, bf16[2,8,8,64,256]{4,3,2,1,0:T(8,128)(2,1)}, u32[]{:S(2)}) copy-start(bf16[2,8,8,64,256]{4,3,2,1,0:T(8,128)(2,1)} %get-tuple-element.16) | copy-start | bytes 12582916
